TPU v7x, 32 devices: a whole 2x2x4 slice. The times are simulated.
32 devices in a mesh: row: 4 (over y, core), col: 8 (over z, x).
Axes of the slice: x: 2, y: 2, z: 4, core: 2. Of those that a mesh axis runs over, the one named last changes fastest.
Arguments:
- inner_base: bfloat16 [4, 1, 2, 4096, 14336], P(None, None, None, 'row', 'col'), may hold values from -250 to 250
- inner_left: bfloat16 [4, 1, 2, 4096, 16], P(None, None, None, ('row', 'col')), may hold values from -6 to 6
- inner_right: bfloat16 [4, 1, 2, 16, 14336], P(None, None, None, 'row', 'col'), may hold values from -12 to 12
- inner_mag: float32 [4, 1, 2, 14336], P(None, None, None, 'col'), may hold values from 512 to 2048
- outer_base: bfloat16 [4, 1, 14336, 4096], P(None, None, 'row', 'col'), may hold values from -250 to 250
- outer_left: bfloat16 [4, 1, 14336, 16], P(None, None, ('row', 'col')), may hold values from -6 to 6
- outer_right: bfloat16 [4, 1, 16, 4096], P(None, None, 'row', 'col'), may hold values from -12 to 12
- outer_mag: float32 [4, 1, 4096], P(None, None, 'col'), may hold values from 1792 to 7168
Outputs:
- inner_merged: bfloat16 [4, 1, 2, 4096, 14336], P(None, None, None, 'row', 'col')
- outer_merged: bfloat16 [4, 1, 14336, 4096], P(None, None, 'row', 'col')
All inputs are finite; a program needn't handle non-finite values.
Results may differ from a plain program's by a relative error of at most 0.001.
Values may be sent and summed in bfloat16 or wider, within the bound.
A program may use at most 256 MiB of HBM per device.

v0:
```python
import functools

import jax
import jax.numpy as jnp
from jax import lax
from jax.experimental import pallas as pl
from jax.experimental.pallas import tpu as pltpu
from jax.sharding import PartitionSpec as P

epsilon = 1e-06
MESH = pl.DeviceIdType.MESH
ANY = pl.BlockSpec(memory_space=pl.ANY)
VMEM = pl.BlockSpec(memory_space=pltpu.VMEM)
GRANT = 18 << 20
SLOTS, PIECES = 4, 2
WIDTHS = (256, 128)
HEIGHTS = (512, 896, 256, 128, 64, 32, 16)


def peers_of(axis, n):
    me = lax.axis_index(axis)
    low, high, half = lax.rem(me, 2), lax.div(me, 2), n // 2
    partner = me + 1 - 2 * low
    ahead = [lax.rem(high + k, half) * 2 + low for k in range(1, half)]
    behind = [lax.rem(high + half - k, half) * 2 + low for k in range(1, half)]
    return me, partner, ahead, behind


def remote(src, dst, send, recv, axis, target):
    return pltpu.make_async_remote_copy(
        src_ref=src, dst_ref=dst, send_sem=send, recv_sem=recv, device_id={axis: target}, device_id_type=MESH
    )


def gather_kernel(rows, cols, il, ol, ir, orr, ib, ob, gil, gol, gir, gor, vib, vob, local, loads, send, recv):
    barrier = pltpu.get_barrier_semaphore()
    places = {"row": peers_of("row", rows), "col": peers_of("col", cols)}
    greeted = 0
    for axis, (_, partner, ahead, _) in places.items():
        for other in [partner, *ahead]:
            pl.semaphore_signal(barrier, inc=1, device_id={axis: other}, device_id_type=MESH)
            greeted += 1
    pl.semaphore_wait(barrier, greeted)
    items = [("row", rows, ir, gir), ("col", cols, il, gil), ("row", rows, orr, gor), ("col", cols, ol, gol)]
    sends, forwards, slot = [], [], 0
    for number, (axis, n, src, dst) in enumerate(items):
        me, partner, ahead, behind = places[axis]
        mine = pltpu.make_async_copy(src, dst.at[me], local.at[number])
        mine.start()
        arrivals = []
        for k, other in enumerate(ahead):
            copy = remote(src, dst.at[me], send.at[slot], recv.at[slot], axis, other)
            copy.start()
            sends.append(copy)
            arrivals.append((slot, behind[k]))
            slot += 1
        copy = remote(src, dst.at[me], send.at[slot], recv.at[slot], axis, partner)
        copy.start()
        sends.append(copy)
        forwards.append((copy, mine))
        slot += 1
        items[number] = (axis, dst, partner, arrivals)
    bases = []
    for number, (src, dst) in enumerate(((ib, vib), (ob, vob))):
        for t in range(src.shape[0]):
            copy = pltpu.make_async_copy(src.at[t], dst.at[t], loads.at[len(bases)])
            copy.start()
            bases.append(copy)
    last = [f for f, _ in forwards]
    for axis, dst, partner, arrivals in items:
        for number, source in arrivals:
            remote(dst.at[source], dst.at[source], send.at[number], recv.at[number], axis, partner).wait_recv()
            copy = remote(dst.at[source], dst.at[source], send.at[slot], recv.at[slot], axis, partner)
            copy.start()
            sends.append(copy)
            last.append(copy)
            slot += 1
    for copy in last:
        copy.wait_recv()
    for copy in sends:
        copy.wait_send()
    for _, mine in forwards:
        mine.wait()
    for copy in bases:
        copy.wait()


def prepare(left, right, lt, r32, t, rank):
    pieces, _, _, piece = left.shape
    for c in range(pieces):
        lt[c * piece : (c + 1) * piece, :] = left[c, t].T
    for c in range(right.shape[0]):
        share = right.shape[2]
        r32[c * share : (c + 1) * share, :] = right[c, t].astype(jnp.float32)


def tiles(rows, cols):
    width = next((w for w in WIDTHS if cols % w == 0), cols)
    height = next(h for h in HEIGHTS if rows % h == 0)
    return height, width


def squares_weight(left, right, base, out, lt, r32, r16, acc):
    count, rows, cols = base.shape
    height, width = tiles(rows, cols)

    @pl.loop(0, count)
    def _(t):
        prepare(left, right, lt, r32, t, r32.shape[0])
        r16[...] = r32[...].astype(jnp.bfloat16)
        for j in range(cols // width):
            part = slice(j * width, (j + 1) * width)

            def add(i, total):
                span = pl.ds(pl.multiple_of(i * height, height), height)
                delta = jnp.dot(lt[span, :], r16[:, part], preferred_element_type=jnp.float32)
                full = base[t, span, part].astype(jnp.float32) + delta
                return total + jnp.sum((full * full).reshape(height // 8, 8, width), axis=0)

            total = lax.fori_loop(0, rows // height, add, jnp.zeros((8, width), jnp.float32), unroll=True)
            acc[:, part] = total
        out[t] = jnp.sum(acc[...], axis=0, keepdims=True)


def squares_kernel(gil, gol, gir, gor, vib, vob, sin, sout, lti, lto, r32i, r32o, r16i, r16o, acci, acco):
    squares_weight(gil, gir, vib, sin, lti, r32i, r16i, acci)
    squares_weight(gol, gor, vob, sout, lto, r32o, r16o, acco)


def factor_kernel(rows, sin, sout, min_, mout, fin, fout, hin, hout, send, recv):
    me = lax.axis_index("row")
    barrier = pltpu.get_barrier_semaphore()
    others = [lax.rem(me + k, rows) for k in range(1, rows)]
    for other in others:
        pl.semaphore_signal(barrier, inc=1, device_id={"row": other}, device_id_type=MESH)
    pl.semaphore_wait(barrier, rows - 1)
    copies = []
    for k, other in enumerate(others):
        for number, (src, held) in enumerate(((sin, hin), (sout, hout))):
            slot = 2 * k + number
            copy = remote(src, held.at[k], send.at[slot], recv.at[slot], "row", other)
            copy.start()
            copies.append(copy)
    for copy in copies:
        copy.wait()
    for src, held, mag, out in ((sin, hin, min_, fin), (sout, hout, mout, fout)):
        total = src[...]
        for k in range(rows - 1):
            total = total + held[k]
        scale = lax.rsqrt(total + epsilon)
        groups = mag.shape[1]
        for t in range(out.shape[0]):
            row = t % groups
            out[t] = mag[t // groups, row : row + 1, :] * scale[t]


def scale_weight(left, right, base, factor, out, lt, r32, r16, stage, sems):
    count, rows, cols = base.shape
    slots, chunk, _ = stage.shape
    pieces = rows // chunk
    height, width = tiles(chunk, cols)

    def store(step):
        slot = lax.rem(step, slots)
        span = pl.ds(pl.multiple_of(lax.rem(step, pieces) * chunk, chunk), chunk)
        return pltpu.make_async_copy(stage.at[slot], out.at[lax.div(step, pieces), span], sems.at[slot])

    @pl.loop(0, count)
    def _(t):
        prepare(left, right, lt, r32, t, r32.shape[0])
        r16[...] = r32[...].astype(jnp.bfloat16)

        @pl.loop(0, pieces)
        def _(p):
            step = t * pieces + p
            slot = lax.rem(step, slots)

            @pl.when(step >= slots)
            def _():
                store(step - slots).wait()

            for j in range(cols // width):
                part = slice(j * width, (j + 1) * width)
                scale = jnp.broadcast_to(factor[t, :, part], (8, width))

                def merge(i, carry):
                    span = pl.ds(pl.multiple_of(p * chunk + i * height, height), height)
                    delta = jnp.dot(lt[span, :], r16[:, part], preferred_element_type=jnp.float32)
                    full = base[t, span, part].astype(jnp.float32) + delta
                    merged = full.reshape(height // 8, 8, width) * scale[None]
                    local = pl.ds(pl.multiple_of(i * height, height), height)
                    stage[slot, local, part] = merged.reshape(height, width).astype(jnp.bfloat16)
                    return carry

                lax.fori_loop(0, chunk // height, merge, 0, unroll=True)
            store(step).start()

    return [store(step) for step in range(count * pieces - slots, count * pieces)]


def scale_kernel(
    gil, gol, gir, gor, vib, vob, fin, fout, oin, oout, lti, lto, r32i, r32o, r16i, r16o, stagei, stageo, semi, semo
):
    stores = scale_weight(gil, gir, vib, fin, oin, lti, r32i, r16i, stagei, semi)
    stores += scale_weight(gol, gor, vob, fout, oout, lto, r32o, r16o, stageo, semo)
    for copy in stores:
        copy.wait()


def pinned(arrays):
    return [pltpu.with_memory_space_constraint(a, pltpu.VMEM) for a in arrays]


def shards(rows, cols, inner_base, inner_left, inner_right, inner_mag, outer_base, outer_left, outer_right, outer_mag):
    rank = inner_left.shape[-1]
    ib = inner_base.reshape((-1, *inner_base.shape[-2:]))
    ob = outer_base.reshape((-1, *outer_base.shape[-2:]))
    il = jnp.swapaxes(inner_left, -1, -2).reshape((-1, rank, inner_left.shape[-2]))
    ol = jnp.swapaxes(outer_left, -1, -2).reshape((-1, rank, outer_left.shape[-2]))
    ir = inner_right.reshape((-1, *inner_right.shape[-2:]))
    orr = outer_right.reshape((-1, *outer_right.shape[-2:]))
    im = inner_mag.reshape((-1, *inner_mag.shape[-2:]))
    om = outer_mag.reshape((ob.shape[0], 1, -1))
    weights, bf16, f32 = ib.shape[0] + ob.shape[0], jnp.bfloat16, jnp.float32
    copies = 4 * (cols + rows)
    gathered = pl.pallas_call(
        functools.partial(gather_kernel, rows, cols),
        out_shape=[
            pltpu.VMEM((n, *a.shape), bf16) for n, a in ((cols, il), (cols, ol), (rows, ir), (rows, orr))
        ] + [pltpu.VMEM(a.shape, bf16) for a in (ib, ob)],
        in_specs=[ANY] * 6,
        out_specs=[VMEM] * 6,
        scratch_shapes=[
            pltpu.SemaphoreType.DMA((4,)),
            pltpu.SemaphoreType.DMA((weights,)),
            pltpu.SemaphoreType.DMA((copies,)),
            pltpu.SemaphoreType.DMA((copies,)),
        ],
        compiler_params=pltpu.CompilerParams(collective_id=0, has_side_effects=True, vmem_limit_bytes=GRANT),
        name="gather",
    )(il, ol, ir, orr, ib, ob)
    gathered = pinned(gathered)
    work = []
    for shape in ((ib.shape[1], rank), (ob.shape[1], rank)):
        work.append(pltpu.VMEM(shape, bf16))
    for kind in (f32, bf16):
        for base in (ib, ob):
            work.append(pltpu.VMEM((rank, base.shape[2]), kind))
    sums = pl.pallas_call(
        squares_kernel,
        out_shape=[pltpu.VMEM((a.shape[0], 1, a.shape[2]), f32) for a in (ib, ob)],
        in_specs=[VMEM] * 6,
        out_specs=[VMEM] * 2,
        scratch_shapes=work + [pltpu.VMEM((8, a.shape[2]), f32) for a in (ib, ob)],
        compiler_params=pltpu.CompilerParams(vmem_limit_bytes=GRANT),
        name="squares",
    )(*gathered)
    sums = pinned(sums)
    factors = pl.pallas_call(
        functools.partial(factor_kernel, rows),
        out_shape=[pltpu.VMEM(s.shape, f32) for s in sums],
        in_specs=[VMEM] * 4,
        out_specs=[VMEM] * 2,
        scratch_shapes=[pltpu.VMEM((rows - 1, *s.shape), f32) for s in sums]
        + [pltpu.SemaphoreType.DMA((2 * rows - 2,))] * 2,
        compiler_params=pltpu.CompilerParams(collective_id=1, has_side_effects=True, vmem_limit_bytes=GRANT),
        name="factor",
    )(*sums, im, om)
    inner, outer = pl.pallas_call(
        scale_kernel,
        out_shape=[jax.ShapeDtypeStruct(a.shape, bf16) for a in (ib, ob)],
        in_specs=[VMEM] * 8,
        out_specs=[ANY] * 2,
        scratch_shapes=work
        + [pltpu.VMEM((SLOTS, a.shape[1] // PIECES, a.shape[2]), bf16) for a in (ib, ob)]
        + [pltpu.SemaphoreType.DMA((SLOTS,))] * 2,
        compiler_params=pltpu.CompilerParams(vmem_limit_bytes=GRANT),
        name="scale",
    )(*gathered, *pinned(factors))
    return inner.reshape(inner_base.shape), outer.reshape(outer_base.shape)


def solution(mesh):
    in_specs = (
        P(None, None, None, "row", "col"),
        P(None, None, None, ("row", "col"), None),
        P(None, None, None, "row", "col"),
        P(None, None, None, "col"),
        P(None, None, "row", "col"),
        P(None, None, ("row", "col"), None),
        P(None, None, "row", "col"),
        P(None, None, "col"),
    )
    out_specs = (P(None, None, None, "row", "col"), P(None, None, "row", "col"))
    body = functools.partial(shards, mesh.shape["row"], mesh.shape["col"])
    return jax.shard_map(body, mesh=mesh, in_specs=in_specs, out_specs=out_specs, check_vma=False)
```

profile of v0, /device:TPU:0, one launch (start us, length us, event | category | flops | bytes accessed | tf_op | source)
XLA Modules:
  0.0 58.9 jit_solution(5620739818494543863)
XLA Ops:
  0.6 19.9 %gather.1 = (bf16[8,8,16,128]{3,2,1,0:T(8,128)(2,1)S(1)}, bf16[8,4,16,448]{3,2,1,0:T(8,128)(2,1)S(1)}, bf16[4,8,4,1792]{3,2,1,0:T(4,128)(2,1)S(1)}, bf16[4,4,4,5...) custom-call(bf16[8,16,128]{2,1,0:T(8,128)(2,1)} %bitcast.24, ...), custom_call_target="tpu_custom_call" | custom-call | tf_op jit(solution)/shard_map/gather/pallas_call | solution.py:226
  20.5 0.0 copy-start
  20.5 0.0 copy-start.1
  20.5 14.9 %squares.1 = (f32[8,1,1792]{2,1,0:T(1,128)S(1)}, f32[4,1,512]{2,1,0:T(1,128)S(1)}) custom-call(bf16[8,8,16,128]{3,2,1,0:T(8,128)(2,1)S(1)} %get-tuple-element.14.gil, bf16[8,4,16,448]{3,2,1,0:T(8,128)(2,1)S(1)} %get-tuple-element.15.gol, bf16[4,8,4,1792]{3,2,1,0:T(4,128)(2,1)S(1)} %get-tuple-element.16.gir, ...), custom_call_target="tpu_custom_call" | custom-call | tf_op jit(solution)/shard_map/squares/pallas_call | solution.py:249
  35.5 0.0 copy-done
  35.5 0.0 copy-done.1
  35.5 5.2 %factor.1 = (f32[8,1,1792]{2,1,0:T(1,128)S(1)}, f32[4,1,512]{2,1,0:T(1,128)S(1)}) custom-call(f32[8,1,1792]{2,1,0:T(1,128)S(1)} %get-tuple-element.20.sin, f32[4,1,512]{2,1,0:T(1,128)S(1)} %get-tuple-element.21.sout, f32[4,2,1792]{2,1,0:T(2,128)S(1)} %bitcast.19, f32[4,1,512]{2,1,0:T(1,128)S(1)} %copy-done.1), custom_call_target="tpu_custom_call" | custom-call | tf_op jit(solution)/shard_map/factor/pallas_call | solution.py:259
  40.7 18.2 %scale.1 = (bf16[8,1024,1792]{2,1,0:T(8,128)(2,1)}, bf16[4,3584,512]{2,1,0:T(8,128)(2,1)}) custom-call(bf16[8,8,16,128]{3,2,1,0:T(8,128)(2,1)S(1)} %get-tuple-element.14.gil, bf16[8,4,16,448]{3,2,1,0:T(8,128)(2,1)S(1)} %get-tuple-element.15.gol, bf16[4,8,4,1792]{3,2,1,0:T(4,128)(2,1)S(1)} %get-tuple-element.16.gir, ...), custom_call_target="tpu_custom_call" | custom-call | tf_op jit(solution)/shard_map/scale/pallas_call | solution.py:269
Async XLA Ops:
  20.5 15.0 %copy-start = (f32[4,1,2,1792]{3,2,1,0:T(2,128)S(1)}, f32[4,1,2,1792]{3,2,1,0:T(2,128)}, u32[]{:S(2)}) copy-start(f32[4,1,2,1792]{3,2,1,0:T(2,128)} %param.11) | copy-start | bytes 172036
  20.5 15.0 %copy-start.1 = (f32[4,1,512]{2,1,0:T(1,128)S(1)}, f32[4,1,512]{2,1,0:T(1,128)}, u32[]{:S(2)}) copy-start(f32[4,1,512]{2,1,0:T(1,128)} %mout.1) | copy-start | bytes 24580
where the time goes:
time: 59.2 us; the launch traced here: 58.9 us
  Pallas kernels  58.2 us (98%)
  between operations  0.68 us (1%)
    pallas_call x1, Pallas kernels, shards(): pl.pallas_call(functools.partial(gather_kernel, rows, cols), out_shape=[p...  19.9 us
    pallas_call x1, Pallas kernels, shards(): pl.pallas_call(scale_kernel, out_shape=[jax.ShapeDtypeStruct(a.shape, bf1...  18.2 us
    pallas_call x1, Pallas kernels, shards(): pl.pallas_call(squares_kernel, out_shape=[pltpu.VMEM((a.shape[0], 1, a.sh...  14.9 us
    pallas_call x1, Pallas kernels, shards(): pl.pallas_call(functools.partial(factor_kernel, rows), out_shape=[pltpu.V...  5.16 us

commit v1 on v0

v1 whole, which is shorter than its diff:
```python
import functools

import jax
import jax.numpy as jnp
from jax import lax
from jax.experimental import pallas as pl
from jax.experimental.pallas import tpu as pltpu
from jax.sharding import PartitionSpec as P

epsilon = 1e-06
MESH = pl.DeviceIdType.MESH
ANY = pl.BlockSpec(memory_space=pl.ANY)
VMEM = pl.BlockSpec(memory_space=pltpu.VMEM)
GRANT = 10 << 20
AHEAD = 4
WIDTHS = (256, 128)
HEIGHTS = (512, 896, 256, 128, 64, 32, 16)


def remote(src, dst, send, recv, axis, target):
    return pltpu.make_async_remote_copy(
        src_ref=src, dst_ref=dst, send_sem=send, recv_sem=recv, device_id={axis: target}, device_id_type=MESH
    )


def tiles(rows, cols):
    width = next((w for w in WIDTHS if cols % w == 0), cols)
    height = next(h for h in HEIGHTS if rows % h == 0)
    return height, width


def group_of(count):
    return 2 if count % 2 == 0 else 1


def prepare(left, right, lt, r16, r32, t):
    pieces, _, _, piece = left.shape
    for c in range(pieces):
        lt[t, c * piece : (c + 1) * piece, :] = left[c, t].T
    share = right.shape[2]
    for c in range(right.shape[0]):
        r32[c * share : (c + 1) * share, :] = right[c, t].astype(jnp.float32)
    r16[t] = r32[...].astype(jnp.bfloat16)


def combined(base, lt, r16, t, span, part):
    delta = jnp.dot(lt[t, span, :], r16[t, :, part], preferred_element_type=jnp.float32)
    return base[t, span, part].astype(jnp.float32) + delta


def squares_weight(base, lt, r16, acc, sums, t):
    _, rows, cols = base.shape
    height, width = tiles(rows, cols)
    for j in range(cols // width):
        part = slice(j * width, (j + 1) * width)
        total = jnp.zeros((8, width), jnp.float32)
        for i in range(rows // height):
            full = combined(base, lt, r16, t, slice(i * height, (i + 1) * height), part)
            total = total + jnp.sum((full * full).reshape(height // 8, 8, width), axis=0)
        acc[:, part] = total
    sums[t] = jnp.sum(acc[...], axis=0, keepdims=True)


def scale_weight(base, lt, r16, factor, t):
    _, rows, cols = base.shape
    height, width = tiles(rows, cols)
    for j in range(cols // width):
        part = slice(j * width, (j + 1) * width)
        scale = jnp.broadcast_to(factor[t, :, part], (8, width))
        for i in range(rows // height):
            span = slice(i * height, (i + 1) * height)
            full = combined(base, lt, r16, t, span, part)
            merged = full.reshape(height // 8, 8, width) * scale[None]
            base[t, span, part] = merged.reshape(height, width).astype(jnp.bfloat16)


def collect_kernel(
    rows, cols,
    il, ol, ir, orr, ib, ob, im, om,
    vib, vob, lti, lto, r16i, r16o, fin, fout,
    gil, gol, gir, gor, r32i, r32o, acci, acco, sumi, sumo, heldi, heldo, mi, mo,
    local, loadi, loado, lsi, lri, lso, lro, rsi, rri, rso, rro, xsi, xri, xso, xro,
):
    me_row, me_col = lax.axis_index("row"), lax.axis_index("col")
    row_others = [lax.rem(me_row + k, rows) for k in range(1, rows)]
    row_back = [lax.rem(me_row + rows - k, rows) for k in range(1, rows)]
    col_others = [lax.rem(me_col + k, cols) for k in range(1, cols)]
    col_back = [lax.rem(me_col + cols - k, cols) for k in range(1, cols)]
    barrier = pltpu.get_barrier_semaphore()
    for axis, others in (("row", row_others), ("col", col_others)):
        for other in others:
            pl.semaphore_signal(barrier, inc=1, device_id={axis: other}, device_id_type=MESH)

    own = []
    for number, (src, dst) in enumerate(
        ((ir, gir.at[me_row]), (il, gil.at[me_col]), (orr, gor.at[me_row]), (ol, gol.at[me_col]), (im, mi), (om, mo))
    ):
        copy = pltpu.make_async_copy(src, dst, local.at[number])
        copy.start()
        own.append(copy)

    def load(kind, t):
        src, dst, sem = (ib, vib, loadi) if kind == 0 else (ob, vob, loado)
        return pltpu.make_async_copy(src.at[t], dst.at[t], sem.at[t])

    order = [(0, t) for t in range(ib.shape[0])] + [(1, t) for t in range(ob.shape[0])]
    for item in order[:AHEAD]:
        load(*item).start()
    pl.semaphore_wait(barrier, rows + cols - 2)
    for copy in own:
        copy.wait()

    kinds = (
        (gil, lsi, lri, gir, rsi, rri, xsi, xri, sumi, heldi, mi, fin),
        (gol, lso, lro, gor, rso, rro, xso, xro, sumo, heldo, mo, fout),
    )

    def shares(kind, t):
        left, ls, lr, right, rs, rr = kinds[kind][:6]
        copies = []
        for k, other in enumerate(row_others):
            piece = right.at[me_row, t]
            copies.append(remote(piece, piece, rs.at[t, k], rr.at[t, k], "row", other))
        for k, other in enumerate(col_others):
            piece = left.at[me_col, t]
            copies.append(remote(piece, piece, ls.at[t, k], lr.at[t, k], "col", other))
        return copies

    def arrivals(kind, t):
        left, ls, lr, right, rs, rr = kinds[kind][:6]
        copies = []
        for k, other in enumerate(row_back):
            piece = right.at[other, t]
            copies.append(remote(piece, piece, rs.at[t, k], rr.at[t, k], "row", other))
        for k, other in enumerate(col_back):
            piece = left.at[other, t]
            copies.append(remote(piece, piece, ls.at[t, k], lr.at[t, k], "col", other))
        return copies

    def exchange(kind, t):
        xs, xr, sums, held = kinds[kind][6:10]
        return [
            remote(sums.at[t], held.at[k, t], xs.at[t, k], xr.at[t, k], "row", other)
            for k, other in enumerate(row_others)
        ]

    for kind, count in ((0, ib.shape[0]), (1, ob.shape[0])):

        @pl.loop(0, count)
        def _(t):
            for copy in shares(kind, t):
                copy.start()

    for item in order[AHEAD : AHEAD + 2]:
        load(*item).start()
    waiting = order[AHEAD + 2 :]

    def finish(kind, t):
        xs, xr, sums, held, mag, out = kinds[kind][6:]
        for copy in exchange(kind, t):
            copy.wait_recv()
        total = sums[t]
        for k in range(rows - 1):
            total = total + held[k, t]
        groups = mag.shape[1]
        if groups == 1:
            strength = mag[t]
        else:
            layer, place = lax.div(t, groups), lax.rem(t, groups)
            strength = mag[layer, pl.ds(place, 1), :]
        out[t] = strength * lax.rsqrt(total + epsilon)

    bodies = (
        (vib, lti, r16i, r32i, acci, sumi, gil, gir),
        (vob, lto, r16o, r32o, acco, sumo, gol, gor),
    )
    for kind in (0, 1):
        base, lt, r16, r32, acc, sums, left, right = bodies[kind]
        count = base.shape[0]
        group = group_of(count)
        if kind == 1:
            last = ib.shape[0]
            for t in range(last - group_of(last), last):
                for copy in exchange(0, t):
                    copy.start()

        @pl.loop(0, count // group)
        def _(p):
            first = p * group
            for u in range(group):
                load(kind, first + u).wait()
                for copy in arrivals(kind, first + u):
                    copy.wait_recv()
            done = (0 if kind == 0 else ib.shape[0])
            for u in range(group):
                position = done + first + u
                for number, item in enumerate(waiting):

                    @pl.when(position == number)
                    def _():
                        load(*item).start()

            @pl.when(p > 0)
            def _():
                for u in range(group):
                    for copy in exchange(kind, first - group + u):
                        copy.start()

            for u in range(group):
                prepare(left, right, lt, r16, r32.at[u], first + u)
            for u in range(group):
                squares_weight(base, lt, r16, acc.at[u], sums, first + u)

    count = ob.shape[0]
    early = group_of(ib.shape[0])
    for t in range(early):
        finish(0, t)
    for t in range(count - group_of(count), count):
        for copy in exchange(1, t):
            copy.start()
    for t in range(early):
        scale_weight(vib, lti, r16i, fin, t)

    @pl.loop(early, ib.shape[0])
    def _(t):
        finish(0, t)

    @pl.loop(0, count)
    def _(t):
        finish(1, t)

    for kind, total in ((0, ib.shape[0]), (1, ob.shape[0])):

        @pl.loop(0, total)
        def _(t):
            for copy in shares(kind, t):
                copy.wait_send()
            for copy in exchange(kind, t):
                copy.wait_send()


def scale_kernel(lti, lto, r16i, r16o, fin, fout, ibase, obase, oin, oout, vib, vob, semi, semo):
    early = group_of(vib.shape[0])

    def store(src, dst, sem, t):
        return pltpu.make_async_copy(src.at[t], dst.at[t], sem.at[t])

    for t in range(early):
        store(vib, oin, semi, t).start()
    for base, lt, r16, factor, out, sem, begin in (
        (vib, lti, r16i, fin, oin, semi, early),
        (vob, lto, r16o, fout, oout, semo, 0),
    ):
        count = base.shape[0]
        group = group_of(count)

        @pl.loop(begin // group, count // group)
        def _(p):
            for u in range(group):
                scale_weight(base, lt, r16, factor, p * group + u)
            for u in range(group):
                store(base, out, sem, p * group + u).start()

    for base, out, sem in ((vib, oin, semi), (vob, oout, semo)):

        @pl.loop(0, base.shape[0])
        def _(t):
            store(base, out, sem, t).wait()


def pinned(arrays):
    return [pltpu.with_memory_space_constraint(a, pltpu.VMEM) for a in arrays]


def shards(rows, cols, inner_base, inner_left, inner_right, inner_mag, outer_base, outer_left, outer_right, outer_mag):
    rank = inner_left.shape[-1]
    ib = inner_base.reshape((-1, *inner_base.shape[-2:]))
    ob = outer_base.reshape((-1, *outer_base.shape[-2:]))
    il = jnp.swapaxes(inner_left, -1, -2).reshape((-1, rank, inner_left.shape[-2]))
    ol = jnp.swapaxes(outer_left, -1, -2).reshape((-1, rank, outer_left.shape[-2]))
    ir = inner_right.reshape((-1, *inner_right.shape[-2:]))
    orr = outer_right.reshape((-1, *outer_right.shape[-2:]))
    im = inner_mag.reshape((-1, *inner_mag.shape[-2:]))
    om = outer_mag.reshape((ob.shape[0], 1, -1))
    bf16, f32, dma = jnp.bfloat16, jnp.float32, pltpu.SemaphoreType.DMA
    bases = (ib, ob)
    counts = (ib.shape[0], ob.shape[0])
    scratch = [pltpu.VMEM((n, *a.shape), bf16) for n, a in ((cols, il), (cols, ol), (rows, ir), (rows, orr))]
    scratch += [pltpu.VMEM((group_of(b.shape[0]), rank, b.shape[2]), f32) for b in bases]
    scratch += [pltpu.VMEM((group_of(b.shape[0]), 8, b.shape[2]), f32) for b in bases]
    scratch += [pltpu.VMEM((b.shape[0], 1, b.shape[2]), f32) for b in bases]
    scratch += [pltpu.VMEM((rows - 1, b.shape[0], 1, b.shape[2]), f32) for b in bases]
    scratch += [pltpu.VMEM(m.shape, f32) for m in (im, om)]
    scratch += [dma((6,))] + [dma((n,)) for n in counts]
    for width in (cols - 1, rows - 1, rows - 1):
        for n in counts:
            scratch += [dma((n, width))] * 2
    held = [pltpu.VMEM(b.shape, bf16) for b in bases]
    lefts = [pltpu.VMEM((b.shape[0], b.shape[1], rank), bf16) for b in bases]
    rights = [pltpu.VMEM((b.shape[0], rank, b.shape[2]), bf16) for b in bases]
    factors = [pltpu.VMEM((b.shape[0], 1, b.shape[2]), f32) for b in bases]
    vib, vob, *rest = pinned(
        pl.pallas_call(
            functools.partial(collect_kernel, rows, cols),
            out_shape=held + lefts + rights + factors,
            in_specs=[ANY] * 8,
            out_specs=[VMEM] * 8,
            scratch_shapes=scratch,
            compiler_params=pltpu.CompilerParams(collective_id=0, has_side_effects=True, vmem_limit_bytes=GRANT),
            name="collect",
        )(il, ol, ir, orr, ib, ob, im, om)
    )
    inner, outer, _, _ = pl.pallas_call(
        scale_kernel,
        out_shape=[jax.ShapeDtypeStruct(b.shape, bf16) for b in bases] + held,
        in_specs=[VMEM] * 8,
        out_specs=[ANY] * 2 + [VMEM] * 2,
        input_output_aliases={6: 2, 7: 3},
        scratch_shapes=[dma((n,)) for n in counts],
        compiler_params=pltpu.CompilerParams(vmem_limit_bytes=GRANT),
        name="scale",
    )(*rest, vib, vob)
    return inner.reshape(inner_base.shape), outer.reshape(outer_base.shape)


def solution(mesh):
    in_specs = (
        P(None, None, None, "row", "col"),
        P(None, None, None, ("row", "col"), None),
        P(None, None, None, "row", "col"),
        P(None, None, None, "col"),
        P(None, None, "row", "col"),
        P(None, None, ("row", "col"), None),
        P(None, None, "row", "col"),
        P(None, None, "col"),
    )
    out_specs = (P(None, None, None, "row", "col"), P(None, None, "row", "col"))
    body = functools.partial(shards, mesh.shape["row"], mesh.shape["col"])
    return jax.shard_map(body, mesh=mesh, in_specs=in_specs, out_specs=out_specs, check_vma=False)
```

time: 59.2 us -> 51.3 us (0.87)
  Pallas kernels: 58.2 us -> 50.5 us
    pallas_call x4 -> x2, Pallas kernels: 58.2 us -> 50.5 us  [the longest x1 36.2 us: shards(): pl.pallas_call(functools.partial(collect_kernel, rows, cols), out_shape=h...]
where the time goes in v1:
time: 51.3 us; the launch traced here: 51.2 us
  Pallas kernels  50.5 us (98%)
  between operations  0.64 us (1%)
    pallas_call x1, Pallas kernels, shards(): pl.pallas_call(functools.partial(collect_kernel, rows, cols), out_shape=h...  36.2 us
    pallas_call x1, Pallas kernels, shards(): pl.pallas_call(scale_kernel, out_shape=[jax.ShapeDtypeStruct(b.shape, bf1...  14.3 us

profile of v1, /device:TPU:0, one launch (start us, length us, event | category | flops | bytes accessed | tf_op | source)
XLA Modules:
  0.0 51.2 jit_solution(14782349150236058822)
XLA Ops:
  0.6 36.2 %collect.1 = (bf16[8,1024,1792]{2,1,0:T(8,128)(2,1)S(1)}, bf16[4,3584,512]{2,1,0:T(8,128)(2,1)S(1)}, bf16[8,1024,16]{2,1,0:T(8,128)(2,1)S(1)}, bf16[4,3584,16]{2...) custom-call(bf16[8,16,128]{2,1,0:T(8,128)(2,1)} %bitcast.24, ...), custom_call_target="tpu_custom_call" | custom-call | tf_op jit(solution)/shard_map/collect/pallas_call | solution.py:303
  36.9 14.3 %scale.1 = (bf16[8,1024,1792]{2,1,0:T(8,128)(2,1)}, bf16[4,3584,512]{2,1,0:T(8,128)(2,1)}, bf16[8,1024,1792]{2,1,0:T(8,128)(2,1)S(1)}, bf16[4,3584,512]{2,1,0:T(8,128)(2,1)S(1)}) custom-call(bf16[8,1024,16]{2,1,0:T(8,128)(2,1)S(1)} %get-tuple-element.12.lti, ...), custom_call_target="tpu_custom_call", output_to_operand_aliasing={{2}: (6, {}), {3}: (7, {})} | custom-call | tf_op jit(solution)/shard_map/scale/pallas_call | solution.py:313

commit v2 on v1

v2 whole, which is shorter than its diff:
```python
import functools

import jax
import jax.numpy as jnp
from jax import lax
from jax.experimental import pallas as pl
from jax.experimental.pallas import tpu as pltpu
from jax.sharding import PartitionSpec as P

epsilon = 1e-06
MESH = pl.DeviceIdType.MESH
ANY = pl.BlockSpec(memory_space=pl.ANY)
VMEM = pl.BlockSpec(memory_space=pltpu.VMEM)
GRANT = 10 << 20
AHEAD = 3
WIDTHS = (256, 128)
HEIGHTS = (512, 896, 256, 128, 64, 32, 16)


def remote(src, dst, send, recv, axis, target):
    return pltpu.make_async_remote_copy(
        src_ref=src, dst_ref=dst, send_sem=send, recv_sem=recv, device_id={axis: target}, device_id_type=MESH
    )


def tiles(rows, cols):
    width = next((w for w in WIDTHS if cols % w == 0), cols)
    height = next(h for h in HEIGHTS if rows % h == 0)
    return height, width


def group_of(count):
    return 2 if count % 2 == 0 else 1


def blocks(count, first, size):
    edges = [0, *range(min(first, count), count, size), count]
    return [(begin, end) for begin, end in zip(edges, edges[1:])]


def plans(inner, outer):
    work = [blocks(inner, 2, 3), blocks(outer, 2, 2)]
    return work, [blocks(inner, 2, max(inner, 1)), work[1]]


def peers_of(axis, n):
    me = lax.axis_index(axis)
    low, high, half = lax.rem(me, 2), lax.div(me, 2), n // 2
    partner = me + 1 - 2 * low
    ahead = [lax.rem(high + k, half) * 2 + low for k in range(1, half)]
    behind = [lax.rem(high + half - k, half) * 2 + low for k in range(1, half)]
    return me, partner, ahead, behind


def prepare(left, right, lt, r16, r32, t):
    pieces, _, _, piece = left.shape
    for c in range(pieces):
        lt[t, c * piece : (c + 1) * piece, :] = left[c, t].T
    share = right.shape[2]
    for c in range(right.shape[0]):
        r32[c * share : (c + 1) * share, :] = right[c, t].astype(jnp.float32)
    r16[t] = r32[...].astype(jnp.bfloat16)


def combined(base, lt, r16, t, span, part):
    delta = jnp.dot(lt[t, span, :], r16[t, :, part], preferred_element_type=jnp.float32)
    return base[t, span, part].astype(jnp.float32) + delta


def squares_weight(base, lt, r16, sums, t):
    _, rows, cols = base.shape
    height, width = tiles(rows, cols)
    for j in range(cols // width):
        part = slice(j * width, (j + 1) * width)
        total = jnp.zeros((8, width), jnp.float32)
        for i in range(rows // height):
            full = combined(base, lt, r16, t, slice(i * height, (i + 1) * height), part)
            total = total + jnp.sum((full * full).reshape(height // 8, 8, width), axis=0)
        sums[t, :, part] = jnp.sum(total, axis=0, keepdims=True)


def scale_weight(base, lt, r16, factor, t):
    _, rows, cols = base.shape
    height, width = tiles(rows, cols)
    for j in range(cols // width):
        part = slice(j * width, (j + 1) * width)
        scale = jnp.broadcast_to(factor[t, :, part], (8, width))
        for i in range(rows // height):
            span = slice(i * height, (i + 1) * height)
            full = combined(base, lt, r16, t, span, part)
            merged = full.reshape(height // 8, 8, width) * scale[None]
            base[t, span, part] = merged.reshape(height, width).astype(jnp.bfloat16)


def collect_kernel(
    rows, cols,
    il, ol, ir, orr, ib, ob, im, om,
    vib, vob, lti, lto, r16i, r16o, fin, fout,
    gil, gol, gir, gor, r32i, r32o, sumi, sumo, heldi, heldo, mi, mo,
    local, sent, loadi, loado, nearli, farli, nearlo, farlo, nearri, farri, nearro, farro, xi, xo,
):
    places = {"row": peers_of("row", rows), "col": peers_of("col", cols)}
    me_row, me_col = places["row"][0], places["col"][0]
    row_others = [lax.rem(me_row + k, rows) for k in range(1, rows)]
    barrier = pltpu.get_barrier_semaphore()
    greeted = [("row", other) for other in row_others]
    greeted += [("col", other) for other in [places["col"][1], *places["col"][2]]]
    for axis, other in greeted:
        pl.semaphore_signal(barrier, inc=1, device_id={axis: other}, device_id_type=MESH)

    own = []
    for number, (src, dst) in enumerate(
        ((ir, gir.at[me_row]), (il, gil.at[me_col]), (orr, gor.at[me_row]), (ol, gol.at[me_col]), (im, mi), (om, mo))
    ):
        copy = pltpu.make_async_copy(src, dst, local.at[number])
        copy.start()
        own.append(copy)

    inner, outer = ib.shape[0], ob.shape[0]
    work, cuts = plans(inner, outer)
    flows = (
        {"row": (gir, sent.at[0], nearri, farri), "col": (gil, sent.at[1], nearli, farli)},
        {"row": (gor, sent.at[2], nearro, farro), "col": (gol, sent.at[3], nearlo, farlo)},
    )
    bodies = (
        (ib, vib, loadi, lti, r16i, r32i, gil, gir, sumi, heldi, xi, sent.at[4], mi, fin),
        (ob, vob, loado, lto, r16o, r32o, gol, gor, sumo, heldo, xo, sent.at[5], mo, fout),
    )

    def load(kind, number):
        src, dst, sems = bodies[kind][:3]
        begin, end = work[kind][number]
        span = pl.ds(begin, end - begin)
        whole = pltpu.make_async_copy(src.at[span], dst.at[span], sems.at[number])
        return [pltpu.make_async_copy(src.at[t], dst.at[t], sems.at[number]) for t in range(begin, end)], whole

    def pieces(kind, number, axis, sources, sem):
        data, send, _, _ = flows[kind][axis]
        begin, end = cuts[kind][number]
        place = data.at[sources, pl.ds(begin, end - begin)]
        return remote(place, place, send, sem, axis, places[axis][1])

    def shares(kind, number):
        begin, end = cuts[kind][number]
        for axis in ("row", "col"):
            data, send, near, far = flows[kind][axis]
            me, partner, ahead, _ = places[axis]
            piece = data.at[me, pl.ds(begin, end - begin)]
            for other in ahead:
                remote(piece, piece, send, near.at[number], axis, other).start()
            remote(piece, piece, send, far.at[number], axis, partner).start()

    def forward(kind, number):
        for axis in ("row", "col"):
            _, _, near, far = flows[kind][axis]
            behind = places[axis][3]
            if behind:
                pieces(kind, number, axis, pl.ds(0, len(behind)), near.at[number]).wait_recv()
            for source in behind:
                pieces(kind, number, axis, source, far.at[number]).start()

    def landed(kind, number):
        for axis in ("row", "col"):
            _, _, _, far = flows[kind][axis]
            pieces(kind, number, axis, pl.ds(0, len(places[axis][3]) + 1), far.at[number]).wait_recv()

    def exchange(kind, number):
        sums, held, sems, send = bodies[kind][8:12]
        for t in range(*work[kind][number]):
            for k, other in enumerate(row_others):
                remote(sums.at[t], held.at[k, t], send, sems.at[number], "row", other).start()

    def finish(kind, number):
        sums, held, sems, send, mag, out = bodies[kind][8:]
        begin, end = work[kind][number]
        place = held.at[:, pl.ds(begin, end - begin)]
        remote(place, place, send, sems.at[number], "row", row_others[0]).wait_recv()
        for t in range(begin, end):
            total = sums[t]
            for k in range(rows - 1):
                total = total + held[k, t]
            layer, place = divmod(t, mag.shape[1])
            out[t] = mag[layer, place : place + 1, :] * lax.rsqrt(total + epsilon)

    pl.semaphore_wait(barrier, len(greeted))
    for copy in own:
        copy.wait()
    for kind in (0, 1):
        for number in range(len(cuts[kind])):
            shares(kind, number)
    order = [(kind, number) for kind in (0, 1) for number in range(len(work[kind]))]
    for item in order[:AHEAD]:
        for copy in load(*item)[0]:
            copy.start(priority=1)
    for number in range(len(cuts[0])):
        forward(0, number)

    for place, (kind, number) in enumerate(order):
        begin, end = work[kind][number]
        load(kind, number)[1].wait()
        for group, cut in enumerate(cuts[kind]):
            if cut[0] == begin:
                landed(kind, group)
        for group in range(len(cuts[1])):
            if place == min(1 + group, len(work[0]) - 1):
                forward(1, group)
        if place + AHEAD < len(order):
            for copy in load(*order[place + AHEAD])[0]:
                copy.start(priority=1)
        if place > 0:
            exchange(*order[place - 1])
        if place > 1:
            finish(*order[place - 2])
        _, base, _, lt, r16, r32, left, right, sums = bodies[kind][:9]
        for t in range(begin, end):
            prepare(left, right, lt, r16, r32.at[t - begin], t)
            squares_weight(base, lt, r16, sums, t)

    if len(order) > 1:
        finish(*order[-2])
    exchange(*order[-1])
    for t in range(work[0][0][1]):
        scale_weight(vib, lti, r16i, fin, t)
    finish(*order[-1])

    for kind in (0, 1):
        for axis in ("row", "col"):
            data, send, near, _ = flows[kind][axis]
            place = data.at[pl.ds(0, data.shape[0] - 1)]
            remote(place, place, send, near.at[0], axis, places[axis][1]).wait_send()
        held, sems, send = bodies[kind][9:12]
        remote(held, held, send, sems.at[0], "row", row_others[0]).wait_send()


def scale_kernel(lti, lto, r16i, r16o, fin, fout, ibase, obase, oin, oout, vib, vob, sems):
    early = plans(vib.shape[0], vob.shape[0])[0][0][0][1]
    for t in range(early):
        pltpu.make_async_copy(vib.at[t], oin.at[t], sems.at[0]).start()
    for number, (base, lt, r16, factor, out, begin) in enumerate(
        ((vib, lti, r16i, fin, oin, early), (vob, lto, r16o, fout, oout, 0))
    ):
        group = group_of(base.shape[0] - begin)

        @pl.loop(0, (base.shape[0] - begin) // group)
        def _(p):
            first = begin + p * group
            for u in range(group):
                scale_weight(base, lt, r16, factor, first + u)
            for u in range(group):
                pltpu.make_async_copy(base.at[first + u], out.at[first + u], sems.at[number]).start()

    pltpu.make_async_copy(vib, oin, sems.at[0]).wait()
    pltpu.make_async_copy(vob, oout, sems.at[1]).wait()


def pinned(arrays):
    return [pltpu.with_memory_space_constraint(a, pltpu.VMEM) for a in arrays]


def shards(rows, cols, inner_base, inner_left, inner_right, inner_mag, outer_base, outer_left, outer_right, outer_mag):
    rank = inner_left.shape[-1]
    ib = inner_base.reshape((-1, *inner_base.shape[-2:]))
    ob = outer_base.reshape((-1, *outer_base.shape[-2:]))
    il = jnp.swapaxes(inner_left, -1, -2).reshape((-1, rank, inner_left.shape[-2]))
    ol = jnp.swapaxes(outer_left, -1, -2).reshape((-1, rank, outer_left.shape[-2]))
    ir = inner_right.reshape((-1, *inner_right.shape[-2:]))
    orr = outer_right.reshape((-1, *outer_right.shape[-2:]))
    im = inner_mag.reshape((-1, *inner_mag.shape[-2:]))
    om = outer_mag.reshape((ob.shape[0], 1, -1))
    bf16, f32, dma = jnp.bfloat16, jnp.float32, pltpu.SemaphoreType.DMA
    bases = (ib, ob)
    work, cuts = plans(ib.shape[0], ob.shape[0])
    scratch = [pltpu.VMEM((n, *a.shape), bf16) for n, a in ((cols, il), (cols, ol), (rows, ir), (rows, orr))]
    for b, edges in zip(bases, work):
        scratch.append(pltpu.VMEM((max(end - begin for begin, end in edges), rank, b.shape[2]), f32))
    scratch += [pltpu.VMEM((b.shape[0], 1, b.shape[2]), f32) for b in bases]
    scratch += [pltpu.VMEM((rows - 1, b.shape[0], 1, b.shape[2]), f32) for b in bases]
    scratch += [pltpu.VMEM(m.shape, f32) for m in (im, om)]
    scratch += [dma((6,)), dma((6,))] + [dma((len(edges),)) for edges in work]
    for _ in range(2):
        for edges in cuts:
            scratch += [dma((len(edges),))] * 2
    scratch += [dma((len(edges),)) for edges in work]
    held = [pltpu.VMEM(b.shape, bf16) for b in bases]
    lefts = [pltpu.VMEM((b.shape[0], b.shape[1], rank), bf16) for b in bases]
    rights = [pltpu.VMEM((b.shape[0], rank, b.shape[2]), bf16) for b in bases]
    factors = [pltpu.VMEM((b.shape[0], 1, b.shape[2]), f32) for b in bases]
    vib, vob, *rest = pinned(
        pl.pallas_call(
            functools.partial(collect_kernel, rows, cols),
            out_shape=held + lefts + rights + factors,
            in_specs=[ANY] * 8,
            out_specs=[VMEM] * 8,
            scratch_shapes=scratch,
            compiler_params=pltpu.CompilerParams(collective_id=0, has_side_effects=True, vmem_limit_bytes=GRANT),
            name="collect",
        )(il, ol, ir, orr, ib, ob, im, om)
    )
    inner, outer, _, _ = pl.pallas_call(
        scale_kernel,
        out_shape=[jax.ShapeDtypeStruct(b.shape, bf16) for b in bases] + held,
        in_specs=[VMEM] * 8,
        out_specs=[ANY] * 2 + [VMEM] * 2,
        input_output_aliases={6: 2, 7: 3},
        scratch_shapes=[dma((2,))],
        compiler_params=pltpu.CompilerParams(vmem_limit_bytes=GRANT),
        name="scale",
    )(*rest, vib, vob)
    return inner.reshape(inner_base.shape), outer.reshape(outer_base.shape)


def solution(mesh):
    in_specs = (
        P(None, None, None, "row", "col"),
        P(None, None, None, ("row", "col"), None),
        P(None, None, None, "row", "col"),
        P(None, None, None, "col"),
        P(None, None, "row", "col"),
        P(None, None, ("row", "col"), None),
        P(None, None, "row", "col"),
        P(None, None, "col"),
    )
    out_specs = (P(None, None, None, "row", "col"), P(None, None, "row", "col"))
    body = functools.partial(shards, mesh.shape["row"], mesh.shape["col"])
    return jax.shard_map(body, mesh=mesh, in_specs=in_specs, out_specs=out_specs, check_vma=False)
```

time: 51.3 us -> 45 us (0.88)
  Pallas kernels: 50.5 us -> 44 us
    pallas_call x1, Pallas kernels: 36.2 us -> 29.8 us  [shards(): pl.pallas_call(functools.partial(collect_kernel, rows, cols), out_shape=h...]
where the time goes in v2:
time: 45 us; the launch traced here: 44.8 us
  Pallas kernels  44 us (98%)
  between operations  0.8 us (2%)
    pallas_call x1, Pallas kernels, shards(): pl.pallas_call(functools.partial(collect_kernel, rows, cols), out_shape=h...  29.8 us
    pallas_call x1, Pallas kernels, shards(): pl.pallas_call(scale_kernel, out_shape=[jax.ShapeDtypeStruct(b.shape, bf1...  14.2 us

profile of v2, /device:TPU:0, one launch (start us, length us, event | category | flops | bytes accessed | tf_op | source)
XLA Modules:
  0.0 44.8 jit_solution(897646814950256724)
XLA Ops:
  0.6 29.8 %collect.1 = (bf16[8,1024,1792]{2,1,0:T(8,128)(2,1)S(1)}, bf16[4,3584,512]{2,1,0:T(8,128)(2,1)S(1)}, bf16[8,1024,16]{2,1,0:T(8,128)(2,1)S(1)}, bf16[4,3584,16]{2...) custom-call(bf16[8,16,128]{2,1,0:T(8,128)(2,1)} %bitcast.24, ...), custom_call_target="tpu_custom_call" | custom-call | tf_op jit(solution)/shard_map/collect/pallas_call | solution.py:289
  30.5 14.2 %scale.1 = (bf16[8,1024,1792]{2,1,0:T(8,128)(2,1)}, bf16[4,3584,512]{2,1,0:T(8,128)(2,1)}, bf16[8,1024,1792]{2,1,0:T(8,128)(2,1)S(1)}, bf16[4,3584,512]{2,1,0:T(8,128)(2,1)S(1)}) custom-call(bf16[8,1024,16]{2,1,0:T(8,128)(2,1)S(1)} %get-tuple-element.12.lti, ...), custom_call_target="tpu_custom_call", output_to_operand_aliasing={{2}: (6, {}), {3}: (7, {})} | custom-call | tf_op jit(solution)/shard_map/scale/pallas_call | solution.py:299

commit v3 on v2

--- a/solution.py
+++ b/solution.py
@@ -14,7 +14,6 @@
 GRANT = 10 << 20
 AHEAD = 3
 WIDTHS = (256, 128)
-HEIGHTS = (512, 896, 256, 128, 64, 32, 16)
 
 
 def remote(src, dst, send, recv, axis, target):
@@ -23,10 +22,8 @@
     )
 
 
-def tiles(rows, cols):
-    width = next((w for w in WIDTHS if cols % w == 0), cols)
-    height = next(h for h in HEIGHTS if rows % h == 0)
-    return height, width
+def width_of(cols):
+    return next((w for w in WIDTHS if cols % w == 0), cols)
 
 
 def group_of(count):
@@ -52,51 +49,65 @@
     return me, partner, ahead, behind
 
 
-def prepare(left, right, lt, r16, r32, t):
-    pieces, _, _, piece = left.shape
-    for c in range(pieces):
-        lt[t, c * piece : (c + 1) * piece, :] = left[c, t].T
+def sources_of(cols):
+    me, partner, _, behind = peers_of("col", cols)
+    return [me, *behind, partner, *(source + partner - me for source in behind)]
+
+
+def slots_of(cols):
+    me, half = lax.axis_index("col"), cols // 2
+    low, high = lax.rem(me, 2), lax.div(me, 2)
+    return [lax.rem(high + half - c // 2, half) + half * lax.rem(low + c, 2) for c in range(cols)]
+
+
+def prepare_left(left, lt, t, sources, slots):
+    for k in slots:
+        lt[t, k] = left[sources[k], t].T
+
+
+def prepare_right(right, r16, r32, t):
     share = right.shape[2]
     for c in range(right.shape[0]):
         r32[c * share : (c + 1) * share, :] = right[c, t].astype(jnp.float32)
     r16[t] = r32[...].astype(jnp.bfloat16)
 
 
-def combined(base, lt, r16, t, span, part):
-    delta = jnp.dot(lt[t, span, :], r16[t, :, part], preferred_element_type=jnp.float32)
+def combined(base, lt, r16, t, span, slot, part):
+    delta = jnp.dot(lt[t, slot], r16[t, :, part], preferred_element_type=jnp.float32)
     return base[t, span, part].astype(jnp.float32) + delta
 
 
-def squares_weight(base, lt, r16, sums, t):
-    _, rows, cols = base.shape
-    height, width = tiles(rows, cols)
+def squares_weight(base, lt, r16, t, sources, slots, totals, save):
+    piece, cols = lt.shape[2], base.shape[2]
+    width = width_of(cols)
     for j in range(cols // width):
         part = slice(j * width, (j + 1) * width)
-        total = jnp.zeros((8, width), jnp.float32)
-        for i in range(rows // height):
-            full = combined(base, lt, r16, t, slice(i * height, (i + 1) * height), part)
-            total = total + jnp.sum((full * full).reshape(height // 8, 8, width), axis=0)
-        sums[t, :, part] = jnp.sum(total, axis=0, keepdims=True)
-
-
-def scale_weight(base, lt, r16, factor, t):
-    _, rows, cols = base.shape
-    height, width = tiles(rows, cols)
+        total = jnp.zeros((8, width), jnp.float32) if totals is None else totals[:, part]
+        for k in slots:
+            span = pl.ds(pl.multiple_of(sources[k] * piece, piece), piece)
+            full = combined(base, lt, r16, t, span, k, part)
+            total = total + jnp.sum((full * full).reshape(piece // 8, 8, width), axis=0)
+        save(part, total)
+
+
+def scale_weight(base, lt, r16, factor, t, slots):
+    piece, cols = lt.shape[2], base.shape[2]
+    width = width_of(cols)
     for j in range(cols // width):
         part = slice(j * width, (j + 1) * width)
         scale = jnp.broadcast_to(factor[t, :, part], (8, width))
-        for i in range(rows // height):
-            span = slice(i * height, (i + 1) * height)
-            full = combined(base, lt, r16, t, span, part)
-            merged = full.reshape(height // 8, 8, width) * scale[None]
-            base[t, span, part] = merged.reshape(height, width).astype(jnp.bfloat16)
+        for c, slot in enumerate(slots):
+            span = slice(c * piece, (c + 1) * piece)
+            full = combined(base, lt, r16, t, span, slot, part)
+            merged = full.reshape(piece // 8, 8, width) * scale[None]
+            base[t, span, part] = merged.reshape(piece, width).astype(jnp.bfloat16)
 
 
 def collect_kernel(
     rows, cols,
     il, ol, ir, orr, ib, ob, im, om,
     vib, vob, lti, lto, r16i, r16o, fin, fout,
-    gil, gol, gir, gor, r32i, r32o, sumi, sumo, heldi, heldo, mi, mo,
+    gil, gol, gir, gor, r32i, r32o, acc, sumi, sumo, heldi, heldo, mi, mo,
     local, sent, loadi, loado, nearli, farli, nearlo, farlo, nearri, farri, nearro, farro, xi, xo,
 ):
     places = {"row": peers_of("row", rows), "col": peers_of("col", cols)}
@@ -142,27 +153,30 @@
 
     def shares(kind, number):
         begin, end = cuts[kind][number]
-        for axis in ("row", "col"):
+        for axis in ("col", "row"):
             data, send, near, far = flows[kind][axis]
             me, partner, ahead, _ = places[axis]
             piece = data.at[me, pl.ds(begin, end - begin)]
             for other in ahead:
                 remote(piece, piece, send, near.at[number], axis, other).start()
-            remote(piece, piece, send, far.at[number], axis, partner).start()
+            arrival = near if axis == "col" else far
+            remote(piece, piece, send, arrival.at[number], axis, partner).start()
 
     def forward(kind, number):
-        for axis in ("row", "col"):
+        for axis in ("col", "row"):
             _, _, near, far = flows[kind][axis]
             behind = places[axis][3]
-            if behind:
-                pieces(kind, number, axis, pl.ds(0, len(behind)), near.at[number]).wait_recv()
+            direct = len(behind) + (1 if axis == "col" else 0)
+            if direct:
+                pieces(kind, number, axis, pl.ds(0, direct), near.at[number]).wait_recv()
             for source in behind:
                 pieces(kind, number, axis, source, far.at[number]).start()
 
-    def landed(kind, number):
-        for axis in ("row", "col"):
-            _, _, _, far = flows[kind][axis]
-            pieces(kind, number, axis, pl.ds(0, len(places[axis][3]) + 1), far.at[number]).wait_recv()
+    def landed(kind, number, axis):
+        _, _, _, far = flows[kind][axis]
+        relayed = len(places[axis][3]) + (0 if axis == "col" else 1)
+        if relayed:
+            pieces(kind, number, axis, pl.ds(0, relayed), far.at[number]).wait_recv()
 
     def exchange(kind, number):
         sums, held, sems, send = bodies[kind][8:12]
@@ -192,18 +206,24 @@
     for item in order[:AHEAD]:
         for copy in load(*item)[0]:
             copy.start(priority=1)
-    for number in range(len(cuts[0])):
-        forward(0, number)
+    forward(0, 0)
+    sources = sources_of(cols)
+    direct, relayed = range(cols // 2 + 1), range(cols // 2 + 1, cols)
+    ready = set()
+    pending = [(0, number) for number in range(1, len(cuts[0]))] + [(1, number) for number in range(len(cuts[1]))]
 
     for place, (kind, number) in enumerate(order):
         begin, end = work[kind][number]
+        _, base, _, lt, r16, r32, left, right, sums = bodies[kind][:9]
+        split = kind == 0 and place < len(cuts[0])
         load(kind, number)[1].wait()
-        for group, cut in enumerate(cuts[kind]):
-            if cut[0] == begin:
-                landed(kind, group)
-        for group in range(len(cuts[1])):
-            if place == min(1 + group, len(work[0]) - 1):
-                forward(1, group)
+        while pending and not split:
+            forward(*pending.pop(0))
+        arrived = [group for group, cut in enumerate(cuts[kind]) if cut[0] == begin]
+        for group in arrived:
+            landed(kind, group, "row")
+            if not split:
+                landed(kind, group, "col")
         if place + AHEAD < len(order):
             for copy in load(*order[place + AHEAD])[0]:
                 copy.start(priority=1)
@@ -211,16 +231,47 @@
             exchange(*order[place - 1])
         if place > 1:
             finish(*order[place - 2])
-        _, base, _, lt, r16, r32, left, right, sums = bodies[kind][:9]
+        ahead = order[place + 1] if place + 1 < len(order) and order[place + 1][0] == 1 and not pending else None
+
+        def whole(t):
+            def save(part, total):
+                sums[t, :, part] = jnp.sum(total, axis=0, keepdims=True)
+
+            return save
+
+        def partial(u):
+            def save(part, total):
+                acc[u, :, part] = total
+
+            return save
+
         for t in range(begin, end):
-            prepare(left, right, lt, r16, r32.at[t - begin], t)
-            squares_weight(base, lt, r16, sums, t)
+            prepare_right(right, r16, r32.at[t - begin], t)
+            if split:
+                prepare_left(left, lt, t, sources, direct)
+                squares_weight(base, lt, r16, t, sources, direct, None, partial(t - begin))
+                continue
+            prepare_left(left, lt, t, sources, relayed if (kind, t) in ready else range(cols))
+            if t == begin and ahead is not None:
+                for later in range(*work[1][ahead[1]]):
+                    prepare_left(gol, lto, later, sources, direct)
+                    ready.add((1, later))
+            squares_weight(base, lt, r16, t, sources, range(cols), None, whole(t))
+        if not split:
+            continue
+        if pending:
+            forward(*pending.pop(0))
+        for group in arrived:
+            landed(kind, group, "col")
+        for t in range(begin, end):
+            prepare_left(left, lt, t, sources, relayed)
+            squares_weight(base, lt, r16, t, sources, relayed, acc.at[t - begin], whole(t))
 
     if len(order) > 1:
         finish(*order[-2])
     exchange(*order[-1])
     for t in range(work[0][0][1]):
-        scale_weight(vib, lti, r16i, fin, t)
+        scale_weight(vib, lti, r16i, fin, t, slots_of(cols))
     finish(*order[-1])
 
     for kind in (0, 1):
@@ -232,7 +283,8 @@
         remote(held, held, send, sems.at[0], "row", row_others[0]).wait_send()
 
 
-def scale_kernel(lti, lto, r16i, r16o, fin, fout, ibase, obase, oin, oout, vib, vob, sems):
+def scale_kernel(cols, lti, lto, r16i, r16o, fin, fout, ibase, obase, oin, oout, vib, vob, sems):
+    slots = slots_of(cols)
     early = plans(vib.shape[0], vob.shape[0])[0][0][0][1]
     for t in range(early):
         pltpu.make_async_copy(vib.at[t], oin.at[t], sems.at[0]).start()
@@ -245,7 +297,7 @@
         def _(p):
             first = begin + p * group
             for u in range(group):
-                scale_weight(base, lt, r16, factor, first + u)
+                scale_weight(base, lt, r16, factor, first + u, slots)
             for u in range(group):
                 pltpu.make_async_copy(base.at[first + u], out.at[first + u], sems.at[number]).start()
 
@@ -273,6 +325,7 @@
     scratch = [pltpu.VMEM((n, *a.shape), bf16) for n, a in ((cols, il), (cols, ol), (rows, ir), (rows, orr))]
     for b, edges in zip(bases, work):
         scratch.append(pltpu.VMEM((max(end - begin for begin, end in edges), rank, b.shape[2]), f32))
+    scratch.append(pltpu.VMEM((max(end - begin for begin, end in work[0]), 8, ib.shape[2]), f32))
     scratch += [pltpu.VMEM((b.shape[0], 1, b.shape[2]), f32) for b in bases]
     scratch += [pltpu.VMEM((rows - 1, b.shape[0], 1, b.shape[2]), f32) for b in bases]
     scratch += [pltpu.VMEM(m.shape, f32) for m in (im, om)]
@@ -282,7 +335,7 @@
             scratch += [dma((len(edges),))] * 2
     scratch += [dma((len(edges),)) for edges in work]
     held = [pltpu.VMEM(b.shape, bf16) for b in bases]
-    lefts = [pltpu.VMEM((b.shape[0], b.shape[1], rank), bf16) for b in bases]
+    lefts = [pltpu.VMEM((b.shape[0], cols, b.shape[1] // cols, rank), bf16) for b in bases]
     rights = [pltpu.VMEM((b.shape[0], rank, b.shape[2]), bf16) for b in bases]
     factors = [pltpu.VMEM((b.shape[0], 1, b.shape[2]), f32) for b in bases]
     vib, vob, *rest = pinned(
@@ -297,7 +350,7 @@
         )(il, ol, ir, orr, ib, ob, im, om)
     )
     inner, outer, _, _ = pl.pallas_call(
-        scale_kernel,
+        functools.partial(scale_kernel, cols),
         out_shape=[jax.ShapeDtypeStruct(b.shape, bf16) for b in bases] + held,
         in_specs=[VMEM] * 8,
         out_specs=[ANY] * 2 + [VMEM] * 2,

time: 45 us -> 43.3 us (0.962)
  Pallas kernels: 44 us -> 42.3 us
    pallas_call x1, Pallas kernels: 29.8 us -> 28.1 us  [shards(): pl.pallas_call(functools.partial(collect_kernel, rows, cols), out_shape=h...]
where the time goes in v3:
time: 43.3 us; the launch traced here: 43.1 us
  Pallas kernels  42.3 us (98%)
  between operations  0.8 us (2%)
    pallas_call x1, Pallas kernels, shards(): pl.pallas_call(functools.partial(collect_kernel, rows, cols), out_shape=h...  28.1 us
    pallas_call x1, Pallas kernels, shards(): pl.pallas_call(functools.partial(scale_kernel, cols), out_shape=[jax.Shap...  14.2 us

profile of v3, /device:TPU:0, one launch (start us, length us, event | category | flops | bytes accessed | tf_op | source)
XLA Modules:
  0.0 43.1 jit_solution(10968259033325898003)
XLA Ops:
  0.6 28.1 %collect.1 = (bf16[8,1024,1792]{2,1,0:T(8,128)(2,1)S(1)}, bf16[4,3584,512]{2,1,0:T(8,128)(2,1)S(1)}, bf16[8,8,128,16]{3,2,1,0:T(8,128)(2,1)S(1)}, bf16[4,8,448,1...) custom-call(bf16[8,16,128]{2,1,0:T(8,128)(2,1)} %bitcast.24, ...), custom_call_target="tpu_custom_call" | custom-call | tf_op jit(solution)/shard_map/collect/pallas_call | solution.py:342
  28.8 14.2 %scale.1 = (bf16[8,1024,1792]{2,1,0:T(8,128)(2,1)}, bf16[4,3584,512]{2,1,0:T(8,128)(2,1)}, bf16[8,1024,1792]{2,1,0:T(8,128)(2,1)S(1)}, bf16[4,3584,512]{2,1,0:T(8,128)(2,1)S(1)}) custom-call(bf16[8,8,128,16]{3,2,1,0:T(8,128)(2,1)S(1)} %get-tuple-element.12.lti, ...), custom_call_target="tpu_custom_call", output_to_operand_aliasing={{2}: (6, {}), {3}: (7, {})} | custom-call | tf_op jit(solution)/shard_map/scale/pallas_call | solution.py:352

commit v4 on v3

--- a/solution.py
+++ b/solution.py
@@ -229,8 +229,8 @@
                 copy.start(priority=1)
         if place > 0:
             exchange(*order[place - 1])
-        if place > 1:
-            finish(*order[place - 2])
+        if place > 2:
+            finish(*order[place - 3])
         ahead = order[place + 1] if place + 1 < len(order) and order[place + 1][0] == 1 and not pending else None
 
         def whole(t):
@@ -267,9 +267,11 @@
             prepare_left(left, lt, t, sources, relayed)
             squares_weight(base, lt, r16, t, sources, relayed, acc.at[t - begin], whole(t))
 
+    if len(order) > 2:
+        finish(*order[-3])
+    exchange(*order[-1])
     if len(order) > 1:
         finish(*order[-2])
-    exchange(*order[-1])
     for t in range(work[0][0][1]):
         scale_weight(vib, lti, r16i, fin, t, slots_of(cols))
     finish(*order[-1])
@@ -283,11 +285,18 @@
         remote(held, held, send, sems.at[0], "row", row_others[0]).wait_send()
 
 
+def store(src, dst, t, sem):
+    half = src.shape[1] // 2
+    for k in range(2):
+        span = pl.ds(k * half, half)
+        pltpu.make_async_copy(src.at[t, span], dst.at[t, span], sem).start(priority=k)
+
+
 def scale_kernel(cols, lti, lto, r16i, r16o, fin, fout, ibase, obase, oin, oout, vib, vob, sems):
     slots = slots_of(cols)
     early = plans(vib.shape[0], vob.shape[0])[0][0][0][1]
     for t in range(early):
-        pltpu.make_async_copy(vib.at[t], oin.at[t], sems.at[0]).start()
+        store(vib, oin, t, sems.at[0])
     for number, (base, lt, r16, factor, out, begin) in enumerate(
         ((vib, lti, r16i, fin, oin, early), (vob, lto, r16o, fout, oout, 0))
     ):
@@ -299,7 +308,7 @@
             for u in range(group):
                 scale_weight(base, lt, r16, factor, first + u, slots)
             for u in range(group):
-                pltpu.make_async_copy(base.at[first + u], out.at[first + u], sems.at[number]).start()
+                store(base, out, first + u, sems.at[number])
 
     pltpu.make_async_copy(vib, oin, sems.at[0]).wait()
     pltpu.make_async_copy(vob, oout, sems.at[1]).wait()

time: 43.3 us -> 42.8 us (0.988)
  no operation moved by 1% of the time
where the time goes in v4:
time: 42.8 us; the launch traced here: 42.7 us
  Pallas kernels  41.9 us (98%)
  between operations  0.8 us (2%)
    pallas_call x1, Pallas kernels, shards(): pl.pallas_call(functools.partial(collect_kernel, rows, cols), out_shape=h...  27.8 us
    pallas_call x1, Pallas kernels, shards(): pl.pallas_call(functools.partial(scale_kernel, cols), out_shape=[jax.Shap...  14.1 us

profile of v4, /device:TPU:0, one launch (start us, length us, event | category | flops | bytes accessed | tf_op | source)
XLA Modules:
  0.0 42.7 jit_solution(8137631994163621332)
XLA Ops:
  0.6 27.8 %collect.1 = (bf16[8,1024,1792]{2,1,0:T(8,128)(2,1)S(1)}, bf16[4,3584,512]{2,1,0:T(8,128)(2,1)S(1)}, bf16[8,8,128,16]{3,2,1,0:T(8,128)(2,1)S(1)}, bf16[4,8,448,1...) custom-call(bf16[8,16,128]{2,1,0:T(8,128)(2,1)} %bitcast.24, ...), custom_call_target="tpu_custom_call" | custom-call | tf_op jit(solution)/shard_map/collect/pallas_call | solution.py:351
  28.4 14.1 %scale.1 = (bf16[8,1024,1792]{2,1,0:T(8,128)(2,1)}, bf16[4,3584,512]{2,1,0:T(8,128)(2,1)}, bf16[8,1024,1792]{2,1,0:T(8,128)(2,1)S(1)}, bf16[4,3584,512]{2,1,0:T(8,128)(2,1)S(1)}) custom-call(bf16[8,8,128,16]{3,2,1,0:T(8,128)(2,1)S(1)} %get-tuple-element.12.lti, ...), custom_call_target="tpu_custom_call", output_to_operand_aliasing={{2}: (6, {}), {3}: (7, {})} | custom-call | tf_op jit(solution)/shard_map/scale/pallas_call | solution.py:361
